TPU v7x, 32 devices: a whole 2x2x4 slice. The times are simulated.
32 devices in a mesh: row: 4 (over y, core), col: 8 (over z, x).
Axes of the slice: x: 2, y: 2, z: 4, core: 2. Of those that a mesh axis runs over, the one named last changes fastest.
Arguments:
- nodes: bfloat16 [32768, 512], P(('row', 'col')), may hold values from -8 to 8
- ln1_gain: float32 [512], replicated, may hold values from 0.25 to 1.75
- w_qkv: bfloat16 [512, 1536], replicated, may hold values from -1 to 1
- w_out: bfloat16 [512, 512], replicated, may hold values from -0.25 to 0.25
- ln2_gain: float32 [512], replicated, may hold values from 0.25 to 1.75
- w_up: bfloat16 [512, 2048], replicated, may hold values from -0.25 to 0.25
- w_down: bfloat16 [2048, 512], replicated, may hold values from -0.125 to 0.125
- adjacency: int32 [32768, 128], P(('row', 'col')), may hold values 0 or 1
- remote_ids: int32 [32, 10], replicated, may hold values from 0 to 255, as said below
- remote_live: int32 [32, 10], replicated, may hold values from 0 to 1, as said below
Outputs:
- updated: bfloat16 [32768, 512], P(('row', 'col'))
Inputs may be any that keep to these rules, and one draw needn't show every extreme that they name: `remote_ids`: every entry of device d's list names a block of another device in d's row or d's column of the mesh; the entries of one list are distinct; at most 1 live entries of one list name blocks of one device, and some list has exactly 1 from one device. `remote_live`: some device has all 10 entries live; every device has 8 or more.
All inputs are finite; a program needn't handle non-finite values. No bound on the sum of `adjacency` on one device may be relied on, other than what follows from the above.
Results may differ from a plain program's by a relative error of at most 0.005.
Values may be sent and summed in bfloat16 or wider, within the bound.
A program may use at most 128 MiB of HBM per device.

v0:
```python
import math
import jax
import jax.numpy as jnp
from jax import lax
from jax.sharding import PartitionSpec as P

HEADS = 8
BLK = 128
CAP = 1
EPS = 1e-05
NEG_FILL = -1e30


def normalize(values, gain):
    values = values.astype(jnp.float32)
    row_mean = jnp.mean(values, axis=-1, keepdims=True)
    centered = values - row_mean
    row_var = jnp.mean(centered * centered, axis=-1, keepdims=True)
    return (centered * lax.rsqrt(row_var + EPS) * gain).astype(jnp.bfloat16)


def attend(queries, local_kv, remote_kv, adj_rows, key_alive):
    row_count = queries.shape[0]
    model_width = queries.shape[1]
    head_dim = model_width // HEADS
    block_count = row_count // BLK
    score_scale = 1.0 / math.sqrt(head_dim)
    query_h = queries.reshape(block_count, BLK, HEADS, head_dim)
    local_keys = local_kv[:, :model_width].reshape(block_count, BLK, HEADS, head_dim)
    local_vals = local_kv[:, model_width:].reshape(block_count, BLK, HEADS, head_dim)
    remote_keys = remote_kv[:, :model_width].reshape(-1, HEADS, head_dim)
    remote_vals = remote_kv[:, model_width:].reshape(-1, HEADS, head_dim)
    local_scores = (
        jnp.einsum("bihd,bjhd->bhij", query_h, local_keys, preferred_element_type=jnp.float32)
        * score_scale
    )
    eye_mask = jnp.arange(BLK)[:, None] == jnp.arange(BLK)[None, :]
    allowed = (adj_rows.reshape(block_count, BLK, BLK) > 0) | eye_mask[None]
    local_scores = jnp.where(allowed[:, None], local_scores, NEG_FILL)
    remote_scores = (
        jnp.einsum("bihd,jhd->bhij", query_h, remote_keys, preferred_element_type=jnp.float32)
        * score_scale
    )
    remote_scores = jnp.where(key_alive[None, None, None, :] > 0, remote_scores, NEG_FILL)
    row_max = jnp.maximum(jnp.max(local_scores, axis=-1), jnp.max(remote_scores, axis=-1))
    local_exp = jnp.exp(local_scores - row_max[..., None])
    remote_exp = jnp.exp(remote_scores - row_max[..., None])
    row_total = jnp.sum(local_exp, axis=-1) + jnp.sum(remote_exp, axis=-1)
    local_probs = (local_exp / row_total[..., None]).astype(jnp.bfloat16)
    remote_probs = (remote_exp / row_total[..., None]).astype(jnp.bfloat16)
    summed = jnp.einsum(
        "bhij,bjhd->bihd", local_probs, local_vals, preferred_element_type=jnp.float32
    )
    summed = summed + jnp.einsum(
        "bhij,jhd->bihd", remote_probs, remote_vals, preferred_element_type=jnp.float32
    )
    return summed.reshape(row_count, model_width).astype(jnp.bfloat16)


def choose_blocks(owner_rows, rank_rows, alive_rows, local_rows, self_index):
    cap_iota = jnp.arange(CAP, dtype=jnp.int32)
    matched = (
        alive_rows[:, None, :]
        & (owner_rows[:, None, :] == self_index)
        & (rank_rows[:, None, :] == cap_iota[None, :, None])
    )
    return jnp.sum(matched.astype(jnp.int32) * local_rows[:, None, :], axis=2)


def outgoing(source, chosen_local, peer_count):
    picked = jnp.take(source, chosen_local.reshape(-1), axis=0, mode="clip")
    return picked.reshape(peer_count, CAP, BLK, source.shape[2])


def shards(
    nodes, ln1_gain, w_qkv, w_out, ln2_gain, w_up, w_down, adjacency, remote_ids, remote_live
):
    model_width = nodes.shape[1]
    node_count = nodes.shape[0]
    local_blocks = node_count // BLK
    slot_count = remote_ids.shape[1]
    row_size = lax.axis_size("row")
    col_size = lax.axis_size("col")
    my_row = lax.axis_index("row")
    my_col = lax.axis_index("col")
    self_index = my_row * col_size + my_col
    normed = normalize(nodes, ln1_gain)
    projected = jnp.dot(normed, w_qkv, preferred_element_type=jnp.float32).astype(jnp.bfloat16)
    queries = projected[:, :model_width]
    keyval = projected[:, model_width:]
    owner_dev = remote_ids // local_blocks
    local_slot = remote_ids % local_blocks
    alive_all = remote_live > 0
    same_owner = owner_dev[:, :, None] == owner_dev[:, None, :]
    slot_iota = jnp.arange(slot_count, dtype=jnp.int32)
    earlier = slot_iota[:, None] < slot_iota[None, :]
    slot_rank = jnp.sum(
        (same_owner & earlier[None] & alive_all[:, :, None]).astype(jnp.int32), axis=1
    )
    row_start = my_row * col_size
    col_pick = choose_blocks(
        lax.dynamic_slice_in_dim(owner_dev, row_start, col_size, 0),
        lax.dynamic_slice_in_dim(slot_rank, row_start, col_size, 0),
        lax.dynamic_slice_in_dim(alive_all, row_start, col_size, 0),
        lax.dynamic_slice_in_dim(local_slot, row_start, col_size, 0),
        self_index,
    )

    def column_of(table):
        return lax.dynamic_index_in_dim(
            table.reshape(row_size, col_size, slot_count), my_col, 1, keepdims=False
        )

    row_pick = choose_blocks(
        column_of(owner_dev),
        column_of(slot_rank),
        column_of(alive_all),
        column_of(local_slot),
        self_index,
    )
    source = normed.reshape(local_blocks, BLK, model_width)
    col_recv = lax.all_to_all(
        outgoing(source, col_pick, col_size), "col", split_axis=0, concat_axis=0, tiled=True
    )
    row_recv = lax.all_to_all(
        outgoing(source, row_pick, row_size), "row", split_axis=0, concat_axis=0, tiled=True
    )
    own_owner = lax.dynamic_index_in_dim(owner_dev, self_index, 0, keepdims=False)
    own_rank = jnp.minimum(
        lax.dynamic_index_in_dim(slot_rank, self_index, 0, keepdims=False), CAP - 1
    )
    own_alive = lax.dynamic_index_in_dim(remote_live, self_index, 0, keepdims=False)
    owner_row = own_owner // col_size
    owner_col = own_owner % col_size
    feature_width = col_recv.shape[3]
    from_col = jnp.take(
        col_recv.reshape(col_size * CAP, BLK, feature_width),
        owner_col * CAP + own_rank,
        axis=0,
        mode="clip",
    )
    from_row = jnp.take(
        row_recv.reshape(row_size * CAP, BLK, feature_width),
        owner_row * CAP + own_rank,
        axis=0,
        mode="clip",
    )
    gathered = jnp.where((owner_row == my_row)[:, None, None], from_col, from_row).reshape(
        slot_count * BLK, feature_width
    )
    remote_kv = jnp.dot(
        gathered, w_qkv[:, model_width:], preferred_element_type=jnp.float32
    ).astype(jnp.bfloat16)
    key_alive = jnp.repeat(own_alive, BLK)
    group_rows = 2 * BLK
    group_count = node_count // group_rows

    def one_group(pieces):
        query_part, kv_part, adj_part = pieces
        return attend(query_part, kv_part, remote_kv, adj_part, key_alive)

    mixed = lax.map(
        one_group,
        (
            queries.reshape(group_count, group_rows, model_width),
            keyval.reshape(group_count, group_rows, 2 * model_width),
            adjacency.reshape(group_count, group_rows, BLK),
        ),
    )
    mixed = mixed.reshape(node_count, model_width)
    residual = nodes.astype(jnp.float32) + jnp.dot(mixed, w_out, preferred_element_type=jnp.float32)
    normed_two = normalize(residual, ln2_gain)
    upward = jnp.dot(normed_two, w_up, preferred_element_type=jnp.float32)
    activated = jax.nn.gelu(upward, approximate=True).astype(jnp.bfloat16)
    return (residual + jnp.dot(activated, w_down, preferred_element_type=jnp.float32)).astype(
        jnp.bfloat16
    )


def solution(mesh):
    return jax.shard_map(
        shards,
        mesh=mesh,
        in_specs=(
            P(("row", "col"), None),
            P(),
            P(),
            P(),
            P(),
            P(),
            P(),
            P(("row", "col"), None),
            P(),
            P(),
        ),
        out_specs=P(("row", "col"), None),
        check_vma=False,
    )
```

profile of v0, /device:TPU:0, one launch (start us, length us, event | category | flops | bytes accessed | tf_op | source)
XLA Modules:
  0.0 227.4 jit_solution(1038354618828412443)
XLA Ops:
  9.1 4.3 %all-to-all-start.1 = ((bf16[4,1,128,512]{3,2,1,0:T(8,128)(2,1)}), bf16[4,1,128,512]{3,2,1,0:T(8,128)(2,1)}, u32[]{:S(2)}, u32[]{:S(2)}) async-start(bf16[4,1,128,512]{3,2,1,0:T(8,128)(2,1)} %bitcast.137), calls=%async_computation.1 | async-start | bytes 1048576 | tf_op jit(solution)/shard_map/all_to_all | solution.py:125
  15.1 7.7 %all-to-all-done.1 = bf16[4,1,128,512]{3,2,1,0:T(8,128)(2,1)} async-done(((bf16[4,1,128,512]{3,2,1,0:T(8,128)(2,1)}), bf16[4,1,128,512]{3,2,1,0:T(8,128)(2,1)}, u32[]{:S(2)}, u32[]{:S(2)}) %all-to-all-start.1) | async-done | bytes 524320 | tf_op jit(solution)/shard_map/all_to_all | solution.py:125
  22.9 6.6 %all-to-all-start = ((bf16[8,1,128,512]{3,2,1,0:T(8,128)(2,1)}), bf16[8,1,128,512]{3,2,1,0:T(8,128)(2,1)S(1)}, u32[]{:S(2)}, u32[]{:S(2)}) async-start(bf16[8,1,128,512]{3,2,1,0:T(8,128)(2,1)} %bitcast.135), calls=%async_computation | async-start | bytes 2097152 | tf_op jit(solution)/shard_map/all_to_all | solution.py:122
  29.4 3.6 %convolution_convert_fusion.1 = bf16[1024,1536]{1,0:T(8,128)(2,1)S(1)} fusion(bf16[1024,512]{0,1:T(8,128)(2,1)} %fusion.34, bf16[512,1536]{1,0:T(8,128)(2,1)} %param.14), kind=kOutput, calls=%fused_computation.50 | convolution fusion | flops 1612185600 | bytes 5767168 | tf_op jit(solution)/shard_map/dot_general | solution.py:88
  39.0 16.1 %all-to-all-done = bf16[8,1,128,512]{3,2,1,0:T(8,128)(2,1)S(1)} async-done(((bf16[8,1,128,512]{3,2,1,0:T(8,128)(2,1)}), bf16[8,1,128,512]{3,2,1,0:T(8,128)(2,1)S(1)}, u32[]{:S(2)}, u32[]{:S(2)}) %all-to-all-start) | async-done | bytes 1048608 | tf_op jit(solution)/shard_map/all_to_all | solution.py:122
  59.0 3.0 %convolution_convert_fusion = bf16[1280,1024]{1,0:T(8,128)(2,1)} fusion(bf16[1280,512]{1,0:T(8,128)(2,1)S(1)} %bitcast_select_fusion, bf16[512,1536]{1,0:T(8,128)(2,1)S(1)} %copy-done.11), kind=kOutput, calls=%fused_computation.49 | convolution fusion | flops 1343488000 | bytes 4980736 | tf_op jit(solution)/shard_map/dot_general | solution.py:151
  62.0 4.4 %copy.136 = bf16[1280,1024]{0,1:T(8,128)(2,1)} copy(bf16[1280,1024]{1,0:T(8,128)(2,1)} %convolution_convert_fusion) | data formatting | bytes 5242880
  66.5 147.2 %while.11 = (s32[]{:T(128)}, bf16[4,256,512]{2,1,0:T(8,128)(2,1)}, bf16[4,256,1024]{2,1,0:T(8,128)(2,1)}, s32[4,256,128]{2,1,0:T(8,128)}, bf16[4,256,512]{2,1,0:...) while((s32[]{:T(128)}, bf16[4,256,512]{2,1,0:T(8,128)(2,1)}, ...), condition=%wide.region_10.11_spmd.clone, body=%wide.region_5.10_spmd.clone.sunk | while | flops 772091904 | bytes 101979416 | solution.py:162
  66.5 3.0 %fusion.88 = (bf16[1280,512]{0,1:T(8,128)(2,1)S(1)}, bf16[1280,512]{0,1:T(8,128)(2,1)}) fusion(bf16[1280,1024]{0,1:T(8,128)(2,1)} %get-tuple-element.212), kind=kLoop, calls=%fused_computation.120.clone.1 | loop fusion | bytes 5242880 | tf_op jit(solution)/shard_map/while/body/eval_jaxpr/slice | solution.py:31
  74.7 6.5 %bitcast_reduce_fusion.2 = (f32[2,8,128]{2,0,1:T(2,128)S(1)}, f32[8,2,128,1280]{3,2,1,0:T(8,128)}) fusion(pred[1280]{0:T(1024)(128)(4,1)S(1)} %broadcast_bitcast_fusion.3, bf16[1280,8,64,1]{0,2,3,1:T(8,128)(2,1)S(1)} %bitcast.127, bf16[2,128,8,64]{1,0,3,2:T(2,128)(2,1)} %reshape.378), kind=kOutput, calls=%fused_computation.6.clone.1 | convolution fusion | flops 343406592 | bytes 12068096 | tf_op jit(solution)/shard_map/while/body/eval_jaxpr/bihd,jhd->bhij/dot_general | solution.py:41
  86.8 6.4 %fusion.92 = f32[2,8,128]{2,0,1:T(2,128)S(1)} fusion(f32[8,2,128,1280]{3,2,1,0:T(8,128)} %get-tuple-element.185, f32[2,8,128]{2,0,1:T(2,128)S(1)} %copy.193, pred[1280]{0:T(1024)(128)(4,1)S(1)} %broadcast_bitcast_fusion.3), kind=kLoop, calls=%fused_computation.10.clone.1 | loop fusion | flops 10483712 | bytes 10503424 | tf_op jit(solution)/shard_map/while/body/eval_jaxpr/reduce_sum | solution.py:48
  93.8 4.2 %fusion.93 = f32[2,128,8,64]{1,3,2,0:T(8,128)} fusion(bf16[1280,8,64,1]{0,2,1,3:T(8,128)(2,1)S(1)} %bitcast.129, f32[8,2,128,1280]{3,2,1,0:T(8,128)S(1)} %copy-done.1, f32[2,8,128]{2,0,1:T(2,128)S(1)} %copy.194, f32[2,8,128]{2,0,1:T(2,128)S(1)} %copy.193, pred[1280]{0:T(1024)(128)(4,1)S(1)} %broadcast_bitcast_fusion.3), kind=kOutput, calls=%fused_computation.15.clone.1 | convolution fusion | flops 348651520 | bytes 12338432 | tf_op jit(solution)/shard_map/while/body/eval_jaxpr/bhij,jhd->bihd/dot_general | solution.py:54
  103.3 3.0 %fusion.88 = (bf16[1280,512]{0,1:T(8,128)(2,1)S(1)}, bf16[1280,512]{0,1:T(8,128)(2,1)}) fusion(bf16[1280,1024]{0,1:T(8,128)(2,1)} %get-tuple-element.212), kind=kLoop, calls=%fused_computation.120.clone.1 | loop fusion | bytes 5242880 | tf_op jit(solution)/shard_map/while/body/eval_jaxpr/slice | solution.py:31
  111.5 6.5 %bitcast_reduce_fusion.2 = (f32[2,8,128]{2,0,1:T(2,128)S(1)}, f32[8,2,128,1280]{3,2,1,0:T(8,128)}) fusion(pred[1280]{0:T(1024)(128)(4,1)S(1)} %broadcast_bitcast_fusion.3, bf16[1280,8,64,1]{0,2,3,1:T(8,128)(2,1)S(1)} %bitcast.127, bf16[2,128,8,64]{1,0,3,2:T(2,128)(2,1)} %reshape.378), kind=kOutput, calls=%fused_computation.6.clone.1 | convolution fusion | flops 343406592 | bytes 12068096 | tf_op jit(solution)/shard_map/while/body/eval_jaxpr/bihd,jhd->bhij/dot_general | solution.py:41
  123.6 6.4 %fusion.92 = f32[2,8,128]{2,0,1:T(2,128)S(1)} fusion(f32[8,2,128,1280]{3,2,1,0:T(8,128)} %get-tuple-element.185, f32[2,8,128]{2,0,1:T(2,128)S(1)} %copy.193, pred[1280]{0:T(1024)(128)(4,1)S(1)} %broadcast_bitcast_fusion.3), kind=kLoop, calls=%fused_computation.10.clone.1 | loop fusion | flops 10483712 | bytes 10503424 | tf_op jit(solution)/shard_map/while/body/eval_jaxpr/reduce_sum | solution.py:48
  130.6 4.2 %fusion.93 = f32[2,128,8,64]{1,3,2,0:T(8,128)} fusion(bf16[1280,8,64,1]{0,2,1,3:T(8,128)(2,1)S(1)} %bitcast.129, f32[8,2,128,1280]{3,2,1,0:T(8,128)S(1)} %copy-done.1, f32[2,8,128]{2,0,1:T(2,128)S(1)} %copy.194, f32[2,8,128]{2,0,1:T(2,128)S(1)} %copy.193, pred[1280]{0:T(1024)(128)(4,1)S(1)} %broadcast_bitcast_fusion.3), kind=kOutput, calls=%fused_computation.15.clone.1 | convolution fusion | flops 348651520 | bytes 12338432 | tf_op jit(solution)/shard_map/while/body/eval_jaxpr/bhij,jhd->bihd/dot_general | solution.py:54
  148.3 6.5 %bitcast_reduce_fusion.2 = (f32[2,8,128]{2,0,1:T(2,128)S(1)}, f32[8,2,128,1280]{3,2,1,0:T(8,128)}) fusion(pred[1280]{0:T(1024)(128)(4,1)S(1)} %broadcast_bitcast_fusion.3, bf16[1280,8,64,1]{0,2,3,1:T(8,128)(2,1)S(1)} %bitcast.127, bf16[2,128,8,64]{1,0,3,2:T(2,128)(2,1)} %reshape.378), kind=kOutput, calls=%fused_computation.6.clone.1 | convolution fusion | flops 343406592 | bytes 12068096 | tf_op jit(solution)/shard_map/while/body/eval_jaxpr/bihd,jhd->bhij/dot_general | solution.py:41
  160.4 6.4 %fusion.92 = f32[2,8,128]{2,0,1:T(2,128)S(1)} fusion(f32[8,2,128,1280]{3,2,1,0:T(8,128)} %get-tuple-element.185, f32[2,8,128]{2,0,1:T(2,128)S(1)} %copy.193, pred[1280]{0:T(1024)(128)(4,1)S(1)} %broadcast_bitcast_fusion.3), kind=kLoop, calls=%fused_computation.10.clone.1 | loop fusion | flops 10483712 | bytes 10503424 | tf_op jit(solution)/shard_map/while/body/eval_jaxpr/reduce_sum | solution.py:48
  167.4 4.2 %fusion.93 = f32[2,128,8,64]{1,3,2,0:T(8,128)} fusion(bf16[1280,8,64,1]{0,2,1,3:T(8,128)(2,1)S(1)} %bitcast.129, f32[8,2,128,1280]{3,2,1,0:T(8,128)S(1)} %copy-done.1, f32[2,8,128]{2,0,1:T(2,128)S(1)} %copy.194, f32[2,8,128]{2,0,1:T(2,128)S(1)} %copy.193, pred[1280]{0:T(1024)(128)(4,1)S(1)} %broadcast_bitcast_fusion.3), kind=kOutput, calls=%fused_computation.15.clone.1 | convolution fusion | flops 348651520 | bytes 12338432 | tf_op jit(solution)/shard_map/while/body/eval_jaxpr/bhij,jhd->bihd/dot_general | solution.py:54
  176.8 3.0 %fusion.88 = (bf16[1280,512]{0,1:T(8,128)(2,1)S(1)}, bf16[1280,512]{0,1:T(8,128)(2,1)}) fusion(bf16[1280,1024]{0,1:T(8,128)(2,1)} %get-tuple-element.212), kind=kLoop, calls=%fused_computation.120.clone.1 | loop fusion | bytes 5242880 | tf_op jit(solution)/shard_map/while/body/eval_jaxpr/slice | solution.py:31
  185.1 6.5 %bitcast_reduce_fusion.2 = (f32[2,8,128]{2,0,1:T(2,128)S(1)}, f32[8,2,128,1280]{3,2,1,0:T(8,128)}) fusion(pred[1280]{0:T(1024)(128)(4,1)S(1)} %broadcast_bitcast_fusion.3, bf16[1280,8,64,1]{0,2,3,1:T(8,128)(2,1)S(1)} %bitcast.127, bf16[2,128,8,64]{1,0,3,2:T(2,128)(2,1)} %reshape.378), kind=kOutput, calls=%fused_computation.6.clone.1 | convolution fusion | flops 343406592 | bytes 12068096 | tf_op jit(solution)/shard_map/while/body/eval_jaxpr/bihd,jhd->bhij/dot_general | solution.py:41
  197.2 6.4 %fusion.92 = f32[2,8,128]{2,0,1:T(2,128)S(1)} fusion(f32[8,2,128,1280]{3,2,1,0:T(8,128)} %get-tuple-element.185, f32[2,8,128]{2,0,1:T(2,128)S(1)} %copy.193, pred[1280]{0:T(1024)(128)(4,1)S(1)} %broadcast_bitcast_fusion.3), kind=kLoop, calls=%fused_computation.10.clone.1 | loop fusion | flops 10483712 | bytes 10503424 | tf_op jit(solution)/shard_map/while/body/eval_jaxpr/reduce_sum | solution.py:48
  204.2 4.2 %fusion.93 = f32[2,128,8,64]{1,3,2,0:T(8,128)} fusion(bf16[1280,8,64,1]{0,2,1,3:T(8,128)(2,1)S(1)} %bitcast.129, f32[8,2,128,1280]{3,2,1,0:T(8,128)S(1)} %copy-done.1, f32[2,8,128]{2,0,1:T(2,128)S(1)} %copy.194, f32[2,8,128]{2,0,1:T(2,128)S(1)} %copy.193, pred[1280]{0:T(1024)(128)(4,1)S(1)} %broadcast_bitcast_fusion.3), kind=kOutput, calls=%fused_computation.15.clone.1 | convolution fusion | flops 348651520 | bytes 12338432 | tf_op jit(solution)/shard_map/while/body/eval_jaxpr/bhij,jhd->bihd/dot_general | solution.py:54
  217.8 8.3 %add_convert_fusion = bf16[1024,512]{0,1:T(8,128)(2,1)S(1)} fusion(f32[1024,512]{0,1:T(8,128)} %copy-done.6, bf16[2048,512]{1,0:T(8,128)(2,1)S(1)} %copy-done, bf16[512,2048]{1,0:T(8,128)(2,1)} %param.17, f32[512]{0:T(512)S(1)} %copy-done.12, f32[1024]{0:T(1024)S(1)} %add_rsqrt_fusion, f32[1024]{0:T(1024)S(1)} %broadcast_multiply_fusion), kind=kOutput, calls=%fused_computation.59 | convolution fusion | flops 4316987392 | bytes 7350272 | tf_op jit(solution)/shard_map/dot_general | solution.py:175
  (186 shorter events, 95.3 us)
Async XLA Ops:
  0.0 217.8 %copy-start = (bf16[2048,512]{1,0:T(8,128)(2,1)S(1)}, bf16[2048,512]{1,0:T(8,128)(2,1)}, u32[]{:S(2)}) copy-start(bf16[2048,512]{1,0:T(8,128)(2,1)} %param.18) | copy-start | bytes 6291460
  0.0 2.2 copy-start.10
  2.2 3.6 %copy-start.9 = (s32[32,10]{0,1:T(8,128)S(1)}, s32[32,10]{0,1:T(8,128)}, u32[]{:S(2)}) copy-start(s32[32,10]{0,1:T(8,128)} %param.20) | copy-start | bytes 3844
  2.2 3.8 %copy-start.8 = (s32[32,10]{0,1:T(8,128)S(1)}, s32[32,10]{0,1:T(8,128)}, u32[]{:S(2)}) copy-start(s32[32,10]{0,1:T(8,128)} %param.21) | copy-start | bytes 3844
  5.8 7.7 %copy-start.7 = (bf16[1024,512]{1,0:T(8,128)(2,1)S(1)}, bf16[1024,512]{1,0:T(8,128)(2,1)}, u32[]{:S(2)}) copy-start(bf16[1024,512]{1,0:T(8,128)(2,1)} %copy.143) | copy-start | bytes 3145732
  9.1 13.7 %all-to-all-start.1 = ((bf16[4,1,128,512]{3,2,1,0:T(8,128)(2,1)}), bf16[4,1,128,512]{3,2,1,0:T(8,128)(2,1)}, u32[]{:S(2)}, u32[]{:S(2)}) async-start(bf16[4,1,128,512]{3,2,1,0:T(8,128)(2,1)} %bitcast.137), calls=%async_computation.1 | async-start | bytes 1048576 | tf_op jit(solution)/shard_map/all_to_all | solution.py:125
  22.9 32.2 %all-to-all-start = ((bf16[8,1,128,512]{3,2,1,0:T(8,128)(2,1)}), bf16[8,1,128,512]{3,2,1,0:T(8,128)(2,1)S(1)}, u32[]{:S(2)}, u32[]{:S(2)}) async-start(bf16[8,1,128,512]{3,2,1,0:T(8,128)(2,1)} %bitcast.135), calls=%async_computation | async-start | bytes 2097152 | tf_op jit(solution)/shard_map/all_to_all | solution.py:122
  56.8 2.2 copy-start.11
  81.2 4.0 %copy-start.2 = (bf16[2,128,8,64]{1,0,3,2:T(2,128)(2,1)S(1)}, bf16[2,128,8,64]{1,0,3,2:T(2,128)(2,1)}, u32[]{:S(2)}) copy-start(bf16[2,128,8,64]{1,0,3,2:T(2,128)(2,1)} %reshape.378) | copy-start | bytes 786436 | tf_op jit(solution)/shard_map/while
  85.2 8.0 %copy-start.3 = (bf16[1280,512]{0,1:T(8,128)(2,1)S(1)}, bf16[1280,512]{0,1:T(8,128)(2,1)}, u32[]{:S(2)}) copy-start(bf16[1280,512]{0,1:T(8,128)(2,1)} %get-tuple-element.183) | copy-start | bytes 3932164 | tf_op jit(solution)/shard_map/while
  86.8 7.0 %copy-start.1 = (f32[8,2,128,1280]{3,2,1,0:T(8,128)S(1)}, f32[8,2,128,1280]{3,2,1,0:T(8,128)}, u32[]{:S(2)}) copy-start(f32[8,2,128,1280]{3,2,1,0:T(8,128)} %get-tuple-element.185) | copy-start | bytes 31457284 | tf_op jit(solution)/shard_map/while
  93.8 4.2 %copy-start.5 = (bf16[256,512]{0,1:T(8,128)(2,1)S(1)}, bf16[256,512]{0,1:T(8,128)(2,1)}, u32[]{:S(2)}) copy-start(bf16[256,512]{0,1:T(8,128)(2,1)} %get-tuple-element.190) | copy-start | bytes 786436 | tf_op jit(solution)/shard_map/while
  118.0 4.0 %copy-start.2 = (bf16[2,128,8,64]{1,0,3,2:T(2,128)(2,1)S(1)}, bf16[2,128,8,64]{1,0,3,2:T(2,128)(2,1)}, u32[]{:S(2)}) copy-start(bf16[2,128,8,64]{1,0,3,2:T(2,128)(2,1)} %reshape.378) | copy-start | bytes 786436 | tf_op jit(solution)/shard_map/while
  122.0 8.1 %copy-start.3 = (bf16[1280,512]{0,1:T(8,128)(2,1)S(1)}, bf16[1280,512]{0,1:T(8,128)(2,1)}, u32[]{:S(2)}) copy-start(bf16[1280,512]{0,1:T(8,128)(2,1)} %get-tuple-element.183) | copy-start | bytes 3932164 | tf_op jit(solution)/shard_map/while
  123.6 7.0 %copy-start.1 = (f32[8,2,128,1280]{3,2,1,0:T(8,128)S(1)}, f32[8,2,128,1280]{3,2,1,0:T(8,128)}, u32[]{:S(2)}) copy-start(f32[8,2,128,1280]{3,2,1,0:T(8,128)} %get-tuple-element.185) | copy-start | bytes 31457284 | tf_op jit(solution)/shard_map/while
  130.6 4.2 %copy-start.5 = (bf16[256,512]{0,1:T(8,128)(2,1)S(1)}, bf16[256,512]{0,1:T(8,128)(2,1)}, u32[]{:S(2)}) copy-start(bf16[256,512]{0,1:T(8,128)(2,1)} %get-tuple-element.190) | copy-start | bytes 786436 | tf_op jit(solution)/shard_map/while
  154.8 4.0 %copy-start.2 = (bf16[2,128,8,64]{1,0,3,2:T(2,128)(2,1)S(1)}, bf16[2,128,8,64]{1,0,3,2:T(2,128)(2,1)}, u32[]{:S(2)}) copy-start(bf16[2,128,8,64]{1,0,3,2:T(2,128)(2,1)} %reshape.378) | copy-start | bytes 786436 | tf_op jit(solution)/shard_map/while
  158.8 8.1 %copy-start.3 = (bf16[1280,512]{0,1:T(8,128)(2,1)S(1)}, bf16[1280,512]{0,1:T(8,128)(2,1)}, u32[]{:S(2)}) copy-start(bf16[1280,512]{0,1:T(8,128)(2,1)} %get-tuple-element.183) | copy-start | bytes 3932164 | tf_op jit(solution)/shard_map/while
  160.4 7.0 %copy-start.1 = (f32[8,2,128,1280]{3,2,1,0:T(8,128)S(1)}, f32[8,2,128,1280]{3,2,1,0:T(8,128)}, u32[]{:S(2)}) copy-start(f32[8,2,128,1280]{3,2,1,0:T(8,128)} %get-tuple-element.185) | copy-start | bytes 31457284 | tf_op jit(solution)/shard_map/while
  167.4 4.2 %copy-start.5 = (bf16[256,512]{0,1:T(8,128)(2,1)S(1)}, bf16[256,512]{0,1:T(8,128)(2,1)}, u32[]{:S(2)}) copy-start(bf16[256,512]{0,1:T(8,128)(2,1)} %get-tuple-element.190) | copy-start | bytes 786436 | tf_op jit(solution)/shard_map/while
  191.6 4.0 %copy-start.2 = (bf16[2,128,8,64]{1,0,3,2:T(2,128)(2,1)S(1)}, bf16[2,128,8,64]{1,0,3,2:T(2,128)(2,1)}, u32[]{:S(2)}) copy-start(bf16[2,128,8,64]{1,0,3,2:T(2,128)(2,1)} %reshape.378) | copy-start | bytes 786436 | tf_op jit(solution)/shard_map/while
  195.6 8.1 %copy-start.3 = (bf16[1280,512]{0,1:T(8,128)(2,1)S(1)}, bf16[1280,512]{0,1:T(8,128)(2,1)}, u32[]{:S(2)}) copy-start(bf16[1280,512]{0,1:T(8,128)(2,1)} %get-tuple-element.183) | copy-start | bytes 3932164 | tf_op jit(solution)/shard_map/while
  197.2 7.0 %copy-start.1 = (f32[8,2,128,1280]{3,2,1,0:T(8,128)S(1)}, f32[8,2,128,1280]{3,2,1,0:T(8,128)}, u32[]{:S(2)}) copy-start(f32[8,2,128,1280]{3,2,1,0:T(8,128)} %get-tuple-element.185) | copy-start | bytes 31457284 | tf_op jit(solution)/shard_map/while
  204.2 4.2 %copy-start.5 = (bf16[256,512]{0,1:T(8,128)(2,1)S(1)}, bf16[256,512]{0,1:T(8,128)(2,1)}, u32[]{:S(2)}) copy-start(bf16[256,512]{0,1:T(8,128)(2,1)} %get-tuple-element.190) | copy-start | bytes 786436 | tf_op jit(solution)/shard_map/while
  (3 other events, 4.9 us)
where the time goes:
time: 229 us; the launch traced here: 227 us
  local copies, waits for them, and re-layouts  82.4 us (36%)
  matrix products  74.7 us (33%)
  other arithmetic  35 us (15%)
  waiting for transfers between devices  23.8 us (10%)
  starting transfers between devices  10.8 us (5%)
    dot_general x4, matrix products, attend(): jnp.einsum('bihd,jhd->bhij', query_h, remote_keys, preferred_element_type...  26.2 us
    reduce_sum x8, other arithmetic, attend(): row_total = jnp.sum(local_exp, axis=-1) + jnp.sum(remote_exp, axis=-1)  26.2 us
    dynamic_slice x16, local copies, waits for them, and re-layouts, shards(): lax.map(one_group, (queries.reshape(group_count, group_rows, model_width)...  19.1 us
    dot_general x4, matrix products, attend(): jnp.einsum('bhij,jhd->bihd', remote_probs, remote_vals, preferred_element...  16.9 us
    all_to_all x1, waiting for transfers between devices, shards(): lax.all_to_all(outgoing(source, col_pick, col_size), 'col', split_axis=0,...  16.1 us
    slice x4, local copies, waits for them, and re-layouts, attend(): remote_keys = remote_kv[:, :model_width].reshape(-1, HEADS, head_dim)  11.9 us
    dynamic_update_slice x12, local copies, waits for them, and re-layouts, shards(): lax.map(one_group, (queries.reshape(group_count, group_rows, model_width)...  9.18 us
    dot_general x4, matrix products, attend(): jnp.einsum('bhij,bjhd->bihd', local_probs, local_vals, preferred_element_...  8.63 us
  transfers between devices with their start and end apart: 2, of which 2 were waited for; matrix products, arithmetic and copies ran while one was open for 5% of the time, Pallas kernels for 0%

commit v1 on v0

--- a/solution.py
+++ b/solution.py
@@ -1,3 +1,4 @@
+import functools
 import math
 import jax
 import jax.numpy as jnp
@@ -9,6 +10,36 @@
 CAP = 1
 EPS = 1e-05
 NEG_FILL = -1e30
+
+
+def build_tasks(t0, dimension_no, my_tile):
+    block_next, state_next = (t0.shape[:dimension_no], t0.shape[dimension_no + 1 :])
+    return jnp.moveaxis(t0.reshape(*block_next, my_tile, -1, *state_next), dimension_no, 0)
+
+
+def derive_the_corner(local_values, d_out):
+    local_values = jnp.moveaxis(local_values, 0, d_out)
+    response = local_values.shape
+    return local_values.reshape(
+        *response[:d_out], response[d_out] * response[d_out + 1], *response[d_out + 2 :]
+    )
+
+
+def _expand_sides(state, mesh_ax, q_in, inner_x):
+    mat_out = lax.axis_size(mesh_ax)
+    right_arr, o_now = (mat_out, lax.axis_index(mesh_ax))
+    lower = build_tasks(state, q_in, right_arr)
+    buffer = [lower[o_now]]
+    for pp in [*range(1, right_arr)]:
+        b_now = lower[(o_now + pp) % right_arr]
+        buffer.append(
+            lax.ppermute(b_now, mesh_ax, [(c, (c + pp) % right_arr) for c in range(right_arr)])
+        )
+    lower = jnp.stack(buffer)[(o_now - jnp.arange(right_arr)) % right_arr]
+    return derive_the_corner(lower, inner_x)
+
+
+match_sheets = functools.partial(_expand_sides, mesh_ax="row", q_in=0, inner_x=0)
 
 
 def normalize(values, gain):
@@ -122,9 +153,7 @@
     col_recv = lax.all_to_all(
         outgoing(source, col_pick, col_size), "col", split_axis=0, concat_axis=0, tiled=True
     )
-    row_recv = lax.all_to_all(
-        outgoing(source, row_pick, row_size), "row", split_axis=0, concat_axis=0, tiled=True
-    )
+    row_recv = match_sheets(outgoing(source, row_pick, row_size))
     own_owner = lax.dynamic_index_in_dim(owner_dev, self_index, 0, keepdims=False)
     own_rank = jnp.minimum(
         lax.dynamic_index_in_dim(slot_rank, self_index, 0, keepdims=False), CAP - 1

time: 229 us -> 217 us (0.948)
  waiting for transfers between devices: 23.8 us -> 7.41 us
  local copies, waits for them, and re-layouts: 82.4 us -> 87 us
    all_to_all x1, waiting for transfers between devices: 16.1 us -> 7.4 us  [shards(): lax.all_to_all(outgoing(source, col_pick, col_size), 'col', split_axis=0,...]
    all_to_all x1 -> x0, waiting for transfers between devices: 7.71 us -> none  [shards(): lax.all_to_all(outgoing(source, row_pick, row_size), 'row', split_axis=0,...]
    all_to_all x1 -> x0, starting transfers between devices: 4.27 us -> none  [shards(): lax.all_to_all(outgoing(source, row_pick, row_size), 'row', split_axis=0,...]
    unnamed x20 -> x22, local copies, waits for them, and re-layouts: 7.54 us -> 7.48 us
  transfers between devices with their start and end apart: 2 -> 4, of which waited for: 2 -> 1; matrix products, arithmetic and copies ran while one was open for 5% -> 8% of each run, Pallas kernels for 0% -> 0%
where the time goes in v1:
time: 217 us; the launch traced here: 215 us
  local copies, waits for them, and re-layouts  87 us (40%)
  matrix products  76.3 us (35%)
  other arithmetic  34.7 us (16%)
  starting transfers between devices  9.09 us (4%)
  waiting for transfers between devices  7.41 us (3%)
    dot_general x4, matrix products, attend(): jnp.einsum('bihd,jhd->bhij', query_h, remote_keys, preferred_element_type...  26.2 us
    reduce_sum x8, other arithmetic, attend(): row_total = jnp.sum(local_exp, axis=-1) + jnp.sum(remote_exp, axis=-1)  26.2 us
    dynamic_slice x16, local copies, waits for them, and re-layouts, shards(): lax.map(one_group, (queries.reshape(group_count, group_rows, model_width)...  19.1 us
    dot_general x4, matrix products, attend(): jnp.einsum('bhij,jhd->bihd', remote_probs, remote_vals, preferred_element...  16.9 us
    slice x4, local copies, waits for them, and re-layouts, attend(): remote_keys = remote_kv[:, :model_width].reshape(-1, HEADS, head_dim)  11.9 us
    dynamic_update_slice x12, local copies, waits for them, and re-layouts, shards(): lax.map(one_group, (queries.reshape(group_count, group_rows, model_width)...  9.18 us
    dot_general x4, matrix products, attend(): jnp.einsum('bhij,bjhd->bihd', local_probs, local_vals, preferred_element_...  8.63 us
    dot_general x1, matrix products, shards(): jnp.dot(activated, w_down, preferred_element_type=jnp.float32)  8.26 us
  transfers between devices with their start and end apart: 4, of which 1 were waited for; matrix products, arithmetic and copies ran while one was open for 8% of the time, Pallas kernels for 0%

profile of v1, /device:TPU:0, one launch (start us, length us, event | category | flops | bytes accessed | tf_op | source)
XLA Modules:
  0.0 215.3 jit_solution(1862576431300966368)
XLA Ops:
  9.0 7.3 %all-to-all-start = ((bf16[8,1,128,512]{3,2,1,0:T(8,128)(2,1)}), bf16[8,1,128,512]{3,2,1,0:T(8,128)(2,1)}, u32[]{:S(2)}, u32[]{:S(2)}) async-start(bf16[8,1,128,512]{3,2,1,0:T(8,128)(2,1)} %bitcast.145), calls=%async_computation | async-start | bytes 2097152 | tf_op jit(solution)/shard_map/all_to_all | solution.py:153
  21.5 5.2 %convolution_convert_fusion.1 = bf16[1024,1536]{1,0:T(8,128)(2,1)} fusion(bf16[1024,512]{0,1:T(8,128)(2,1)} %fusion.34, bf16[512,1536]{1,0:T(8,128)(2,1)} %param.14), kind=kOutput, calls=%fused_computation.51 | convolution fusion | flops 1612185600 | bytes 5767168 | tf_op jit(solution)/shard_map/dot_general | solution.py:119
  26.7 3.1 %slice.40 = bf16[1024,1024]{1,0:T(8,128)(2,1)} slice(bf16[1024,1536]{1,0:T(8,128)(2,1)} %convolution_convert_fusion.1), slice={[0:1024], [512:1536]} | slice | bytes 4194304 | tf_op jit(solution)/shard_map/slice | solution.py:121
  34.7 7.4 %all-to-all-done = bf16[8,1,128,512]{3,2,1,0:T(8,128)(2,1)} async-done(((bf16[8,1,128,512]{3,2,1,0:T(8,128)(2,1)}), bf16[8,1,128,512]{3,2,1,0:T(8,128)(2,1)}, u32[]{:S(2)}, u32[]{:S(2)}) %all-to-all-start) | async-done | bytes 1048608 | tf_op jit(solution)/shard_map/all_to_all | solution.py:153
  42.1 3.0 %gather_fusion.1 = bf16[10,128,512]{2,1,0:T(8,128)(2,1)} fusion(bf16[8,128,512]{2,1,0:T(8,128)(2,1)} %bitcast.6, s32[1024]{0:T(1024)S(1)} %pad_clamp_fusion.3), kind=kCustom, calls=%fused_computation.1 | custom fusion | bytes 2621480 | tf_op jit(solution)/shard_map/jit(_take)/gather | solution.py:165
  47.0 3.0 %convolution_convert_fusion = bf16[1280,1024]{1,0:T(8,128)(2,1)} fusion(bf16[1280,512]{1,0:T(8,128)(2,1)S(1)} %bitcast_select_fusion, bf16[512,1536]{1,0:T(8,128)(2,1)S(1)} %copy-done.12), kind=kOutput, calls=%fused_computation.50 | convolution fusion | flops 1343488000 | bytes 4980736 | tf_op jit(solution)/shard_map/dot_general | solution.py:180
  50.0 4.4 %copy.133 = bf16[1280,1024]{0,1:T(8,128)(2,1)} copy(bf16[1280,1024]{1,0:T(8,128)(2,1)} %convolution_convert_fusion) | data formatting | bytes 5242880
  54.4 147.2 %while.11 = (s32[]{:T(128)}, bf16[4,256,512]{2,1,0:T(8,128)(2,1)}, bf16[4,256,1024]{2,1,0:T(8,128)(2,1)}, s32[4,256,128]{2,1,0:T(8,128)}, bf16[4,256,512]{2,1,0:...) while((s32[]{:T(128)}, bf16[4,256,512]{2,1,0:T(8,128)(2,1)}, ...), condition=%wide.region_10.11_spmd.clone, body=%wide.region_5.10_spmd.clone.sunk | while | flops 772091904 | bytes 101979416 | solution.py:191
  54.4 3.0 %fusion.90 = (bf16[1280,512]{0,1:T(8,128)(2,1)S(1)}, bf16[1280,512]{0,1:T(8,128)(2,1)}) fusion(bf16[1280,1024]{0,1:T(8,128)(2,1)} %get-tuple-element.216), kind=kLoop, calls=%fused_computation.133.clone.1 | loop fusion | bytes 5242880 | tf_op jit(solution)/shard_map/while/body/eval_jaxpr/slice | solution.py:62
  62.6 6.5 %bitcast_reduce_fusion.2 = (f32[2,8,128]{2,0,1:T(2,128)S(1)}, f32[8,2,128,1280]{3,2,1,0:T(8,128)}) fusion(pred[1280]{0:T(1024)(128)(4,1)S(1)} %broadcast_bitcast_fusion.3, bf16[1280,8,64,1]{0,2,3,1:T(8,128)(2,1)S(1)} %bitcast.138, bf16[2,128,8,64]{1,0,3,2:T(2,128)(2,1)} %reshape.441), kind=kOutput, calls=%fused_computation.7.clone.1 | convolution fusion | flops 343406592 | bytes 12068096 | tf_op jit(solution)/shard_map/while/body/eval_jaxpr/bihd,jhd->bhij/dot_general | solution.py:72
  74.8 6.4 %fusion.94 = f32[2,8,128]{2,0,1:T(2,128)S(1)} fusion(f32[8,2,128,1280]{3,2,1,0:T(8,128)} %get-tuple-element.189, f32[2,8,128]{2,0,1:T(2,128)S(1)} %copy.190, pred[1280]{0:T(1024)(128)(4,1)S(1)} %broadcast_bitcast_fusion.3), kind=kLoop, calls=%fused_computation.11.clone.1 | loop fusion | flops 10483712 | bytes 10503424 | tf_op jit(solution)/shard_map/while/body/eval_jaxpr/reduce_sum | solution.py:79
  81.7 4.2 %fusion.95 = f32[2,128,8,64]{1,3,2,0:T(8,128)} fusion(bf16[1280,8,64,1]{0,2,1,3:T(8,128)(2,1)S(1)} %bitcast.140, f32[8,2,128,1280]{3,2,1,0:T(8,128)S(1)} %copy-done.1, f32[2,8,128]{2,0,1:T(2,128)S(1)} %copy.191, f32[2,8,128]{2,0,1:T(2,128)S(1)} %copy.190, pred[1280]{0:T(1024)(128)(4,1)S(1)} %broadcast_bitcast_fusion.3), kind=kOutput, calls=%fused_computation.16.clone.1 | convolution fusion | flops 348651520 | bytes 12338432 | tf_op jit(solution)/shard_map/while/body/eval_jaxpr/bhij,jhd->bihd/dot_general | solution.py:85
  91.2 3.0 %fusion.90 = (bf16[1280,512]{0,1:T(8,128)(2,1)S(1)}, bf16[1280,512]{0,1:T(8,128)(2,1)}) fusion(bf16[1280,1024]{0,1:T(8,128)(2,1)} %get-tuple-element.216), kind=kLoop, calls=%fused_computation.133.clone.1 | loop fusion | bytes 5242880 | tf_op jit(solution)/shard_map/while/body/eval_jaxpr/slice | solution.py:62
  99.4 6.5 %bitcast_reduce_fusion.2 = (f32[2,8,128]{2,0,1:T(2,128)S(1)}, f32[8,2,128,1280]{3,2,1,0:T(8,128)}) fusion(pred[1280]{0:T(1024)(128)(4,1)S(1)} %broadcast_bitcast_fusion.3, bf16[1280,8,64,1]{0,2,3,1:T(8,128)(2,1)S(1)} %bitcast.138, bf16[2,128,8,64]{1,0,3,2:T(2,128)(2,1)} %reshape.441), kind=kOutput, calls=%fused_computation.7.clone.1 | convolution fusion | flops 343406592 | bytes 12068096 | tf_op jit(solution)/shard_map/while/body/eval_jaxpr/bihd,jhd->bhij/dot_general | solution.py:72
  111.6 6.4 %fusion.94 = f32[2,8,128]{2,0,1:T(2,128)S(1)} fusion(f32[8,2,128,1280]{3,2,1,0:T(8,128)} %get-tuple-element.189, f32[2,8,128]{2,0,1:T(2,128)S(1)} %copy.190, pred[1280]{0:T(1024)(128)(4,1)S(1)} %broadcast_bitcast_fusion.3), kind=kLoop, calls=%fused_computation.11.clone.1 | loop fusion | flops 10483712 | bytes 10503424 | tf_op jit(solution)/shard_map/while/body/eval_jaxpr/reduce_sum | solution.py:79
  118.5 4.2 %fusion.95 = f32[2,128,8,64]{1,3,2,0:T(8,128)} fusion(bf16[1280,8,64,1]{0,2,1,3:T(8,128)(2,1)S(1)} %bitcast.140, f32[8,2,128,1280]{3,2,1,0:T(8,128)S(1)} %copy-done.1, f32[2,8,128]{2,0,1:T(2,128)S(1)} %copy.191, f32[2,8,128]{2,0,1:T(2,128)S(1)} %copy.190, pred[1280]{0:T(1024)(128)(4,1)S(1)} %broadcast_bitcast_fusion.3), kind=kOutput, calls=%fused_computation.16.clone.1 | convolution fusion | flops 348651520 | bytes 12338432 | tf_op jit(solution)/shard_map/while/body/eval_jaxpr/bhij,jhd->bihd/dot_general | solution.py:85
  128.0 3.0 %fusion.90 = (bf16[1280,512]{0,1:T(8,128)(2,1)S(1)}, bf16[1280,512]{0,1:T(8,128)(2,1)}) fusion(bf16[1280,1024]{0,1:T(8,128)(2,1)} %get-tuple-element.216), kind=kLoop, calls=%fused_computation.133.clone.1 | loop fusion | bytes 5242880 | tf_op jit(solution)/shard_map/while/body/eval_jaxpr/slice | solution.py:62
  136.2 6.5 %bitcast_reduce_fusion.2 = (f32[2,8,128]{2,0,1:T(2,128)S(1)}, f32[8,2,128,1280]{3,2,1,0:T(8,128)}) fusion(pred[1280]{0:T(1024)(128)(4,1)S(1)} %broadcast_bitcast_fusion.3, bf16[1280,8,64,1]{0,2,3,1:T(8,128)(2,1)S(1)} %bitcast.138, bf16[2,128,8,64]{1,0,3,2:T(2,128)(2,1)} %reshape.441), kind=kOutput, calls=%fused_computation.7.clone.1 | convolution fusion | flops 343406592 | bytes 12068096 | tf_op jit(solution)/shard_map/while/body/eval_jaxpr/bihd,jhd->bhij/dot_general | solution.py:72
  148.4 6.4 %fusion.94 = f32[2,8,128]{2,0,1:T(2,128)S(1)} fusion(f32[8,2,128,1280]{3,2,1,0:T(8,128)} %get-tuple-element.189, f32[2,8,128]{2,0,1:T(2,128)S(1)} %copy.190, pred[1280]{0:T(1024)(128)(4,1)S(1)} %broadcast_bitcast_fusion.3), kind=kLoop, calls=%fused_computation.11.clone.1 | loop fusion | flops 10483712 | bytes 10503424 | tf_op jit(solution)/shard_map/while/body/eval_jaxpr/reduce_sum | solution.py:79
  155.3 4.2 %fusion.95 = f32[2,128,8,64]{1,3,2,0:T(8,128)} fusion(bf16[1280,8,64,1]{0,2,1,3:T(8,128)(2,1)S(1)} %bitcast.140, f32[8,2,128,1280]{3,2,1,0:T(8,128)S(1)} %copy-done.1, f32[2,8,128]{2,0,1:T(2,128)S(1)} %copy.191, f32[2,8,128]{2,0,1:T(2,128)S(1)} %copy.190, pred[1280]{0:T(1024)(128)(4,1)S(1)} %broadcast_bitcast_fusion.3), kind=kOutput, calls=%fused_computation.16.clone.1 | convolution fusion | flops 348651520 | bytes 12338432 | tf_op jit(solution)/shard_map/while/body/eval_jaxpr/bhij,jhd->bihd/dot_general | solution.py:85
  173.0 6.5 %bitcast_reduce_fusion.2 = (f32[2,8,128]{2,0,1:T(2,128)S(1)}, f32[8,2,128,1280]{3,2,1,0:T(8,128)}) fusion(pred[1280]{0:T(1024)(128)(4,1)S(1)} %broadcast_bitcast_fusion.3, bf16[1280,8,64,1]{0,2,3,1:T(8,128)(2,1)S(1)} %bitcast.138, bf16[2,128,8,64]{1,0,3,2:T(2,128)(2,1)} %reshape.441), kind=kOutput, calls=%fused_computation.7.clone.1 | convolution fusion | flops 343406592 | bytes 12068096 | tf_op jit(solution)/shard_map/while/body/eval_jaxpr/bihd,jhd->bhij/dot_general | solution.py:72
  185.2 6.4 %fusion.94 = f32[2,8,128]{2,0,1:T(2,128)S(1)} fusion(f32[8,2,128,1280]{3,2,1,0:T(8,128)} %get-tuple-element.189, f32[2,8,128]{2,0,1:T(2,128)S(1)} %copy.190, pred[1280]{0:T(1024)(128)(4,1)S(1)} %broadcast_bitcast_fusion.3), kind=kLoop, calls=%fused_computation.11.clone.1 | loop fusion | flops 10483712 | bytes 10503424 | tf_op jit(solution)/shard_map/while/body/eval_jaxpr/reduce_sum | solution.py:79
  192.1 4.2 %fusion.95 = f32[2,128,8,64]{1,3,2,0:T(8,128)} fusion(bf16[1280,8,64,1]{0,2,1,3:T(8,128)(2,1)S(1)} %bitcast.140, f32[8,2,128,1280]{3,2,1,0:T(8,128)S(1)} %copy-done.1, f32[2,8,128]{2,0,1:T(2,128)S(1)} %copy.191, f32[2,8,128]{2,0,1:T(2,128)S(1)} %copy.190, pred[1280]{0:T(1024)(128)(4,1)S(1)} %broadcast_bitcast_fusion.3), kind=kOutput, calls=%fused_computation.16.clone.1 | convolution fusion | flops 348651520 | bytes 12338432 | tf_op jit(solution)/shard_map/while/body/eval_jaxpr/bhij,jhd->bihd/dot_general | solution.py:85
  205.7 8.3 %add_convert_fusion = bf16[1024,512]{0,1:T(8,128)(2,1)S(1)} fusion(f32[1024,512]{0,1:T(8,128)} %copy-done.6, bf16[2048,512]{1,0:T(8,128)(2,1)S(1)} %copy-done, bf16[512,2048]{1,0:T(8,128)(2,1)} %param.17, f32[512]{0:T(512)S(1)} %copy-done.13, f32[1024]{0:T(1024)S(1)} %add_rsqrt_fusion, f32[1024]{0:T(1024)S(1)} %broadcast_multiply_fusion), kind=kOutput, calls=%fused_computation.60 | convolution fusion | flops 4316987392 | bytes 7350272 | tf_op jit(solution)/shard_map/dot_general | solution.py:204
  (197 shorter events, 95.4 us)
Async XLA Ops:
  0.0 205.7 %copy-start = (bf16[2048,512]{1,0:T(8,128)(2,1)S(1)}, bf16[2048,512]{1,0:T(8,128)(2,1)}, u32[]{:S(2)}) copy-start(bf16[2048,512]{1,0:T(8,128)(2,1)} %param.18) | copy-start | bytes 6291460
  2.2 3.6 %copy-start.9 = (s32[32,10]{0,1:T(8,128)S(1)}, s32[32,10]{0,1:T(8,128)}, u32[]{:S(2)}) copy-start(s32[32,10]{0,1:T(8,128)} %param.21) | copy-start | bytes 3844
  6.1 10.8 %copy-start.7 = (bf16[1024,512]{1,0:T(8,128)(2,1)S(1)}, bf16[1024,512]{1,0:T(8,128)(2,1)}, u32[]{:S(2)}) copy-start(bf16[1024,512]{1,0:T(8,128)(2,1)} %copy.140) | copy-start | bytes 3145732
  9.0 33.2 %all-to-all-start = ((bf16[8,1,128,512]{3,2,1,0:T(8,128)(2,1)}), bf16[8,1,128,512]{3,2,1,0:T(8,128)(2,1)}, u32[]{:S(2)}, u32[]{:S(2)}) async-start(bf16[8,1,128,512]{3,2,1,0:T(8,128)(2,1)} %bitcast.145), calls=%async_computation | async-start | bytes 2097152 | tf_op jit(solution)/shard_map/all_to_all | solution.py:153
  19.4 12.9 %collective-permute-start.2 = (bf16[1,1,128,512]{3,2,1,0:T(8,128)(2,1)S(1)}, bf16[1,1,128,512]{3,2,1,0:T(8,128)(2,1)S(1)}, u32[]{:S(2)}, u32[]{:S(2)}) collective-permute-start(bf16[1,1,128,512]{3,2,1,0:T(8,128)(2,1)S(1)} %get-tuple-element.127), channel_id=1, source_target_pairs={{0,24},{8,0},{16,8},{24,16},{1,25},{9,1},{17,9},{25,17},{2,26},{10... | collective-permute-start | bytes 393224 | tf_op jit(solution)/shard_map/ppermute | solution.py:36
  20.1 12.2 %collective-permute-start.1 = (bf16[1,1,128,512]{3,2,1,0:T(8,128)(2,1)S(1)}, bf16[1,1,128,512]{3,2,1,0:T(8,128)(2,1)S(1)}, u32[]{:S(2)}, u32[]{:S(2)}) collective-permute-start(bf16[1,1,128,512]{3,2,1,0:T(8,128)(2,1)S(1)} %get-tuple-element.125), channel_id=1, source_target_pairs={{0,16},{8,24},{16,0},{24,8},{1,17},{9,25},{17,1},{25,9},{2,18},{10... | collective-permute-start | bytes 393224 | tf_op jit(solution)/shard_map/ppermute | solution.py:36
  21.0 11.3 %collective-permute-start = (bf16[1,1,128,512]{3,2,1,0:T(8,128)(2,1)S(1)}, bf16[1,1,128,512]{3,2,1,0:T(8,128)(2,1)S(1)}, u32[]{:S(2)}, u32[]{:S(2)}) collective-permute-start(bf16[1,1,128,512]{3,2,1,0:T(8,128)(2,1)S(1)} %get-tuple-element.126), channel_id=1, source_target_pairs={{0,8},{8,16},{16,24},{24,0},{1,9},{9,17},{17,25},{25,1},{2,10},{10... | collective-permute-start | bytes 393224 | tf_op jit(solution)/shard_map/ppermute | solution.py:36
  34.7 10.4 %copy-start.8 = (bf16[10,128,512]{2,1,0:T(8,128)(2,1)S(1)}, bf16[10,128,512]{2,1,0:T(8,128)(2,1)}, u32[]{:S(2)}) copy-start(bf16[10,128,512]{2,1,0:T(8,128)(2,1)} %gather_fusion.4) | copy-start | bytes 3932164
  69.2 4.0 %copy-start.2 = (bf16[2,128,8,64]{1,0,3,2:T(2,128)(2,1)S(1)}, bf16[2,128,8,64]{1,0,3,2:T(2,128)(2,1)}, u32[]{:S(2)}) copy-start(bf16[2,128,8,64]{1,0,3,2:T(2,128)(2,1)} %reshape.441) | copy-start | bytes 786436 | tf_op jit(solution)/shard_map/while
  73.2 8.0 %copy-start.3 = (bf16[1280,512]{0,1:T(8,128)(2,1)S(1)}, bf16[1280,512]{0,1:T(8,128)(2,1)}, u32[]{:S(2)}) copy-start(bf16[1280,512]{0,1:T(8,128)(2,1)} %get-tuple-element.187) | copy-start | bytes 3932164 | tf_op jit(solution)/shard_map/while
  74.8 7.0 %copy-start.1 = (f32[8,2,128,1280]{3,2,1,0:T(8,128)S(1)}, f32[8,2,128,1280]{3,2,1,0:T(8,128)}, u32[]{:S(2)}) copy-start(f32[8,2,128,1280]{3,2,1,0:T(8,128)} %get-tuple-element.189) | copy-start | bytes 31457284 | tf_op jit(solution)/shard_map/while
  81.7 4.2 %copy-start.5 = (bf16[256,512]{0,1:T(8,128)(2,1)S(1)}, bf16[256,512]{0,1:T(8,128)(2,1)}, u32[]{:S(2)}) copy-start(bf16[256,512]{0,1:T(8,128)(2,1)} %get-tuple-element.194) | copy-start | bytes 786436 | tf_op jit(solution)/shard_map/while
  106.0 4.0 %copy-start.2 = (bf16[2,128,8,64]{1,0,3,2:T(2,128)(2,1)S(1)}, bf16[2,128,8,64]{1,0,3,2:T(2,128)(2,1)}, u32[]{:S(2)}) copy-start(bf16[2,128,8,64]{1,0,3,2:T(2,128)(2,1)} %reshape.441) | copy-start | bytes 786436 | tf_op jit(solution)/shard_map/while
  110.0 8.1 %copy-start.3 = (bf16[1280,512]{0,1:T(8,128)(2,1)S(1)}, bf16[1280,512]{0,1:T(8,128)(2,1)}, u32[]{:S(2)}) copy-start(bf16[1280,512]{0,1:T(8,128)(2,1)} %get-tuple-element.187) | copy-start | bytes 3932164 | tf_op jit(solution)/shard_map/while
  111.6 7.0 %copy-start.1 = (f32[8,2,128,1280]{3,2,1,0:T(8,128)S(1)}, f32[8,2,128,1280]{3,2,1,0:T(8,128)}, u32[]{:S(2)}) copy-start(f32[8,2,128,1280]{3,2,1,0:T(8,128)} %get-tuple-element.189) | copy-start | bytes 31457284 | tf_op jit(solution)/shard_map/while
  118.5 4.2 %copy-start.5 = (bf16[256,512]{0,1:T(8,128)(2,1)S(1)}, bf16[256,512]{0,1:T(8,128)(2,1)}, u32[]{:S(2)}) copy-start(bf16[256,512]{0,1:T(8,128)(2,1)} %get-tuple-element.194) | copy-start | bytes 786436 | tf_op jit(solution)/shard_map/while
  142.8 4.0 %copy-start.2 = (bf16[2,128,8,64]{1,0,3,2:T(2,128)(2,1)S(1)}, bf16[2,128,8,64]{1,0,3,2:T(2,128)(2,1)}, u32[]{:S(2)}) copy-start(bf16[2,128,8,64]{1,0,3,2:T(2,128)(2,1)} %reshape.441) | copy-start | bytes 786436 | tf_op jit(solution)/shard_map/while
  146.7 8.1 %copy-start.3 = (bf16[1280,512]{0,1:T(8,128)(2,1)S(1)}, bf16[1280,512]{0,1:T(8,128)(2,1)}, u32[]{:S(2)}) copy-start(bf16[1280,512]{0,1:T(8,128)(2,1)} %get-tuple-element.187) | copy-start | bytes 3932164 | tf_op jit(solution)/shard_map/while
  148.4 7.0 %copy-start.1 = (f32[8,2,128,1280]{3,2,1,0:T(8,128)S(1)}, f32[8,2,128,1280]{3,2,1,0:T(8,128)}, u32[]{:S(2)}) copy-start(f32[8,2,128,1280]{3,2,1,0:T(8,128)} %get-tuple-element.189) | copy-start | bytes 31457284 | tf_op jit(solution)/shard_map/while
  155.3 4.2 %copy-start.5 = (bf16[256,512]{0,1:T(8,128)(2,1)S(1)}, bf16[256,512]{0,1:T(8,128)(2,1)}, u32[]{:S(2)}) copy-start(bf16[256,512]{0,1:T(8,128)(2,1)} %get-tuple-element.194) | copy-start | bytes 786436 | tf_op jit(solution)/shard_map/while
  179.6 4.0 %copy-start.2 = (bf16[2,128,8,64]{1,0,3,2:T(2,128)(2,1)S(1)}, bf16[2,128,8,64]{1,0,3,2:T(2,128)(2,1)}, u32[]{:S(2)}) copy-start(bf16[2,128,8,64]{1,0,3,2:T(2,128)(2,1)} %reshape.441) | copy-start | bytes 786436 | tf_op jit(solution)/shard_map/while
  183.5 8.1 %copy-start.3 = (bf16[1280,512]{0,1:T(8,128)(2,1)S(1)}, bf16[1280,512]{0,1:T(8,128)(2,1)}, u32[]{:S(2)}) copy-start(bf16[1280,512]{0,1:T(8,128)(2,1)} %get-tuple-element.187) | copy-start | bytes 3932164 | tf_op jit(solution)/shard_map/while
  185.2 7.0 %copy-start.1 = (f32[8,2,128,1280]{3,2,1,0:T(8,128)S(1)}, f32[8,2,128,1280]{3,2,1,0:T(8,128)}, u32[]{:S(2)}) copy-start(f32[8,2,128,1280]{3,2,1,0:T(8,128)} %get-tuple-element.189) | copy-start | bytes 31457284 | tf_op jit(solution)/shard_map/while
  192.1 4.2 %copy-start.5 = (bf16[256,512]{0,1:T(8,128)(2,1)S(1)}, bf16[256,512]{0,1:T(8,128)(2,1)}, u32[]{:S(2)}) copy-start(bf16[256,512]{0,1:T(8,128)(2,1)} %get-tuple-element.194) | copy-start | bytes 786436 | tf_op jit(solution)/shard_map/while
  (6 other events, 12.5 us)
